TPU v7x, 32 devices: a whole 2x2x4 slice. The times are simulated.
32 devices in a mesh: seq: 8 (over z, y), head: 4 (over x, core).
Axes of the slice: x: 2, y: 2, z: 4, core: 2. Of those that a mesh axis runs over, the one named last changes fastest.
Arguments:
- queries: bfloat16 [4096, 2048], P('seq', 'head'), may hold values from -6 to 6
- key_vectors: bfloat16 [4096, 2048], P('seq', 'head'), may hold values from -6 to 6
- value_vectors: bfloat16 [4096, 2048], P('seq', 'head'), may hold values from -6 to 6
- gate_input: bfloat16 [4096, 2048], P('seq', 'head'), may hold values from -6 to 6
- out_weight: bfloat16 [2048, 4096], P('seq', 'head'), may hold values from -0.125 to 0.125
Outputs:
- layer_output: bfloat16 [4096, 4096], P('seq', 'head')
All inputs are finite; a program needn't handle non-finite values.
Results may differ from a plain program's by a relative error of at most 0.0057.
Values may be sent and summed in bfloat16 or wider, within the bound.
A program may use at most 64 MiB of HBM per device.

v0:
```python
import jax
import jax.numpy as jnp
from jax import lax
from jax.sharding import PartitionSpec as P

HD = 128


def carried_in(shard, axis, combine, identity):
    count, position = (lax.axis_size(axis), lax.axis_index(axis))
    everything = lax.all_gather(shard, axis)
    start = jnp.broadcast_to(jnp.asarray(identity, shard.dtype), shard.shape)

    def turn(k, before):
        reached = k < position
        new = combine(before, everything[k])
        return jnp.where(reached, new, before)

    return lax.fori_loop(0, count, turn, start)


def add_states(earlier, later):
    return earlier + later


def carried(own_state):
    return carried_in(own_state, "seq", add_states, jnp.zeros_like(own_state))


def in_shard(qhead, khead, vhead, scale):
    rows = qhead.shape[0]
    step = min(rows, 512)
    scores = jnp.einsum("thd,shd->hts", qhead, khead, preferred_element_type=jnp.float32) * scale
    rowpos = 0 + lax.broadcasted_iota(jnp.int32, (step, step), 0)
    colpos = lax.broadcasted_iota(jnp.int32, (step, step), 1)
    scores = jnp.where((colpos <= rowpos)[None, :, :], scores, 0.0).astype(jnp.bfloat16)
    pieces = jnp.einsum("hts,she->the", scores, vhead, preferred_element_type=jnp.float32)
    return pieces


def per_device(queries, key_vectors, value_vectors, gate_input, out_weight):
    rows, width = queries.shape
    heads = width // HD
    scale = HD ** (-0.5)
    qhead = queries.reshape(rows, heads, HD)
    khead = key_vectors.reshape(rows, heads, HD)
    vhead = value_vectors.reshape(rows, heads, HD)
    own_state = jnp.einsum("thd,the->hde", khead, vhead, preferred_element_type=jnp.float32)
    local = in_shard(qhead, khead, vhead, scale)
    prefix = carried(own_state)
    inter = (
        jnp.einsum(
            "thd,hde->the", qhead, prefix.astype(jnp.bfloat16), preferred_element_type=jnp.float32
        )
        * scale
    )
    attn = (local + inter).reshape(rows, width)
    squares = jnp.sum(attn * attn, axis=1)
    hidden = (attn * jax.nn.silu(gate_input.astype(jnp.float32))).astype(jnp.bfloat16)
    total = lax.psum(squares, "head")
    features = lax.all_gather(hidden, "head", axis=1, tiled=True)
    full_block = lax.all_gather(out_weight, "seq", axis=0, tiled=True)
    projected = jnp.dot(features, full_block, preferred_element_type=jnp.float32)
    mean_square = total / features.shape[1]
    return (projected * lax.rsqrt(mean_square + 1e-06)[:, None]).astype(jnp.bfloat16)


def solution(mesh):
    placed = (
        P("seq", "head"),
        P("seq", "head"),
        P("seq", "head"),
        P("seq", "head"),
        P("seq", "head"),
    )
    return jax.shard_map(
        per_device, mesh=mesh, in_specs=placed, out_specs=P("seq", "head"), check_vma=False
    )
```

profile of v0, /device:TPU:0, one launch (start us, length us, event | category | flops | bytes accessed | tf_op | source)
XLA Modules:
  0.0 184.2 jit_solution(1914398323355310470)
XLA Ops:
  6.5 1.3 copy.19
  7.9 2.0 %fusion.10 = f32[4,128,128]{2,1,0:T(8,128)} fusion(bf16[512,4,128]{0,2,1:T(8,128)(2,1)S(1)} %bitcast.47, bf16[512,512]{1,0:T(8,128)(2,1)} %param.9), kind=kOutput, calls=%fused_computation.18 | convolution fusion | flops 67108864 | bytes 1310720 | tf_op jit(solution)/shard_map/thd,the->hde/dot_general | solution.py:48
  9.9 0.0 all-gather.5.cloned.1.call-start
  10.0 0.1 iota_compare_fusion
  10.1 51.8 %all-gather.9.cloned.1.call-done = f32[32,128,128]{2,1,0:T(8,128)} async-done(((f32[4,128,128]{2,1,0:T(8,128)}), f32[32,128,128]{2,1,0:T(8,128)}) %all-gather.9.cloned.1.call-update) | async-done | bytes 2097168 | tf_op jit(solution)/shard_map/all_gather | solution.py:11
  61.9 8.5 %while.14 = (s32[]{:T(128)}, f32[4,128,128]{2,1,0:T(8,128)S(1)}, s32[]{:T(128)}, f32[8,4,128,128]{3,2,1,0:T(8,128)}, s32[]{:T(128)}, /*index=5*/s32[]{:T(128)}) while((s32[]{:T(128)}, f32[4,128,128]{2,1,0:T(8,128)S(1)}, s32[]{:T(128)}, f32[8,4,128,128]{3,2,1,0:T(8,128)}, s32[]{:T(128)}, /*index=5*/s32[]{:T(128)}) %tuple.42), condition=%wide.region_1.2_spmd.clone, body=%wide.region_0.1_spmd.clone.sunk | while | flops 196612 | bytes 786525 | solution.py:19
  61.9 1.0 add_select_fusion.2
  62.9 1.0 add_select_fusion.2
  64.0 1.0 add_select_fusion.2
  65.1 1.0 add_select_fusion.2
  66.1 1.0 add_select_fusion.2
  67.2 1.0 add_select_fusion.2
  68.3 1.0 add_select_fusion.2
  69.3 1.0 add_select_fusion.2
  70.4 0.3 fusion.3
  70.7 2.4 %multiply_reduce_fusion = (f32[512]{0:T(512)S(1)}, f32[512,4,128]{0,2,1:T(8,128)S(1)}) fusion(f32[512,4,128]{0,2,1:T(8,128)S(1)} %fusion.3, bf16[512,4,128]{0,2,1:T(8,128)(2,1)S(1)} %bitcast.48, pred[512,512]{1,0:T(8,128)(4,1)S(1)} %iota_compare_fusion, bf16[512,512]{1,0:T(8,128)(2,1)} %param.9, bf16[512,512]{1,0:T(8,128)(2,1)S(1)} %copy-done), kind=kOutput, calls=%fused_computation.14 | convolution fusion | flops 540802560 | bytes 3934208 | tf_op jit(solution)/shard_map/hts,she->the/dot_general | solution.py:37
  73.2 0.3 copy.17
  73.5 0.7 copy-done.1
  74.2 1.1 fusion.8
  75.4 0.7 all-gather.7.cloned.1.call-update
  76.1 5.7 %psum.7 = f32[512]{0:T(512)S(1)} all-reduce(f32[512]{0:T(512)S(1)} %get-tuple-element.108), channel_id=1, replica_groups=mesh['seq'=8,'head'=4] {'head'}, use_global_device_ids=true, to_apply=%region_3.4 | all-reduce | flops 512 | bytes 4096 | tf_op jit(solution)/shard_map/psum | solution.py:60
  81.8 14.8 %all-gather.5.cloned.1.call-done = bf16[512,2048]{1,0:T(8,128)(2,1)} async-done(((bf16[512,512]{1,0:T(8,128)(2,1)}), bf16[512,2048]{1,0:T(8,128)(2,1)}) %all-gather.5.cloned.1.call-update) | async-done | bytes 2097168 | tf_op jit(solution)/shard_map/all_gather | solution.py:61
  96.6 75.0 %all-gather.7.cloned.1.call-done = bf16[2048,1024]{1,0:T(8,128)(2,1)} async-done(((bf16[256,1024]{1,0:T(8,128)(2,1)}), bf16[2048,1024]{1,0:T(8,128)(2,1)}) %all-gather.7.cloned.1.call-update) | async-done | bytes 4194320 | tf_op jit(solution)/shard_map/all_gather | solution.py:62
  171.6 6.1 %multiply_convert_fusion = bf16[512,1024]{1,0:T(8,128)(2,1)} fusion(bf16[512,2048]{1,0:T(8,128)(2,1)} %all-gather.5.cloned.1.call-done, bf16[2048,1024]{1,0:T(8,128)(2,1)} %all-gather.7.cloned.1.call-done, f32[512]{0:T(512)S(1)} %add_rsqrt_fusion), kind=kOutput, calls=%fused_computation.2 | convolution fusion | flops 2148532224 | bytes 7342080 | tf_op jit(solution)/shard_map/dot_general | solution.py:63
  (9 shorter events, 0.1 us)
Async XLA Ops:
  6.5 63.9 %copy-start = (bf16[512,512]{1,0:T(8,128)(2,1)S(1)}, bf16[512,512]{1,0:T(8,128)(2,1)}, u32[]{:S(2)}) copy-start(bf16[512,512]{1,0:T(8,128)(2,1)} %param.7) | copy-start | bytes 1572868
  6.5 55.3 %all-gather.9.cloned.1.call-start = ((), (), s32[]{:S(2)}) async-start(), calls=%async_computation.2 | async-start | bytes 2359296 | tf_op jit(solution)/shard_map/all_gather | solution.py:11
  9.9 86.7 %all-gather.5.cloned.1.call-start = ((), (), s32[]{:S(2)}) async-start(), calls=%async_computation | async-start | bytes 2621440 | tf_op jit(solution)/shard_map/all_gather | solution.py:61
  73.2 1.0 copy-start.1
  75.3 96.2 %all-gather.7.cloned.1.call-start = ((), (), s32[]{:S(2)}) async-start(), calls=%async_computation.1 | async-start | bytes 4718592 | tf_op jit(solution)/shard_map/all_gather | solution.py:62
Sparse Core Ops, SparseCore 0:
  10.0 51.7 all-gather.8
  75.5 21.0 all-gather.4
  98.7 72.7 all-gather.6
where the time goes:
time: 185 us; the launch traced here: 184 us
  waiting for transfers between devices  142 us (77%)
  between operations  13.2 us (7%)
  matrix products  10.9 us (6%)
  other arithmetic  9.53 us (5%)
  blocking collectives  5.67 us (3%)
  local copies, waits for them, and re-layouts  2.34 us (1%)
    all_gather x1, waiting for transfers between devices, per_device(): full_block = lax.all_gather(out_weight, 'seq', axis=0, tiled=True)  75 us
    all_gather x1, waiting for transfers between devices, carried_in(): everything = lax.all_gather(shard, axis)  51.8 us
    all_gather x1, waiting for transfers between devices, per_device(): features = lax.all_gather(hidden, 'head', axis=1, tiled=True)  14.8 us
    select_n x8, other arithmetic, turn(): return jnp.where(reached, new, before)  8.32 us
    dot_general x1, matrix products, per_device(): jnp.dot(features, full_block, preferred_element_type=jnp.float32)  6.12 us
    psum x1, blocking collectives, per_device(): total = lax.psum(squares, 'head')  5.67 us
  transfers between devices with their start and end apart: 3, of which 3 were waited for; matrix products, arithmetic and copies ran while one was open for 0% of the time, Pallas kernels for 0%

commit v1 on v0

--- a/solution.py
+++ b/solution.py
@@ -58,7 +58,12 @@
     squares = jnp.sum(attn * attn, axis=1)
     hidden = (attn * jax.nn.silu(gate_input.astype(jnp.float32))).astype(jnp.bfloat16)
     total = lax.psum(squares, "head")
-    features = lax.all_gather(hidden, "head", axis=1, tiled=True)
+    ring = [hidden]
+    for hop in range(3):
+        ring.append(lax.ppermute(ring[-1], "head", [(dev, (dev + 1) % 4) for dev in range(4)]))
+    features = jnp.roll(
+        jnp.concatenate(ring[::-1], axis=1), (lax.axis_index("head") + 1) * ring[0].shape[1], axis=1
+    )
     full_block = lax.all_gather(out_weight, "seq", axis=0, tiled=True)
     projected = jnp.dot(features, full_block, preferred_element_type=jnp.float32)
     mean_square = total / features.shape[1]

time: 185 us -> 149 us (0.81)
  waiting for transfers between devices: 142 us -> 95.5 us
  local copies, waits for them, and re-layouts: 2.34 us -> 8.81 us
  blocking collectives: 5.67 us -> 9.54 us
    all_gather x1, waiting for transfers between devices: 75 us -> 26.5 us  [per_device(): full_block = lax.all_gather(out_weight, 'seq', axis=0, tiled=True)]
    ppermute x0 -> x3, waiting for transfers between devices: none -> 17.2 us  [per_device(): lax.ppermute(ring[-1], 'head', [(dev, (dev + 1) % 4) for dev in range(4)])]
    all_gather x1 -> x0, waiting for transfers between devices: 14.8 us -> none  [per_device(): features = lax.all_gather(hidden, 'head', axis=1, tiled=True)]
    unnamed x4 -> x9, local copies, waits for them, and re-layouts: 0.7 us -> 6.29 us
    psum x1, blocking collectives: 5.67 us -> 9.54 us  [per_device(): total = lax.psum(squares, 'head')]
  transfers between devices with their start and end apart: 3 -> 5, of which waited for: 3 -> 4; matrix products, arithmetic and copies ran while one was open for 0% -> 14% of each run, Pallas kernels for 0% -> 0%
where the time goes in v1:
time: 149 us; the launch traced here: 148 us
  waiting for transfers between devices  95.5 us (64%)
  between operations  13.5 us (9%)
  matrix products  10.9 us (7%)
  other arithmetic  9.79 us (7%)
  blocking collectives  9.54 us (6%)
  local copies, waits for them, and re-layouts  8.81 us (6%)
    all_gather x1, waiting for transfers between devices, carried_in(): everything = lax.all_gather(shard, axis)  51.1 us
    all_gather x1, waiting for transfers between devices, per_device(): full_block = lax.all_gather(out_weight, 'seq', axis=0, tiled=True)  26.5 us
    ppermute x3, waiting for transfers between devices, per_device(): lax.ppermute(ring[-1], 'head', [(dev, (dev + 1) % 4) for dev in range(4)])  17.2 us
    psum x1, blocking collectives, per_device(): total = lax.psum(squares, 'head')  9.54 us
    select_n x8, other arithmetic, turn(): return jnp.where(reached, new, before)  8.33 us
    unnamed x9, local copies, waits for them, and re-layouts  6.29 us
    dot_general x1, matrix products, per_device(): jnp.dot(features, full_block, preferred_element_type=jnp.float32)  6.12 us
  transfers between devices with their start and end apart: 5, of which 4 were waited for; matrix products, arithmetic and copies ran while one was open for 14% of the time, Pallas kernels for 0%

profile of v1, /device:TPU:0, one launch (start us, length us, event | category | flops | bytes accessed | tf_op | source)
XLA Modules:
  0.0 148.3 jit_solution(16035188707708265485)
XLA Ops:
  6.5 1.3 copy.19
  7.9 2.0 %fusion.14 = f32[4,128,128]{2,1,0:T(8,128)} fusion(bf16[512,4,128]{0,2,1:T(8,128)(2,1)S(1)} %bitcast.46, bf16[512,512]{1,0:T(8,128)(2,1)} %param.9), kind=kOutput, calls=%fused_computation.20 | convolution fusion | flops 67108864 | bytes 1310720 | tf_op jit(solution)/shard_map/thd,the->hde/dot_general | solution.py:48
  10.8 51.1 %all-gather.6.cloned.1.call-done = f32[32,128,128]{2,1,0:T(8,128)} async-done(((f32[4,128,128]{2,1,0:T(8,128)}), f32[32,128,128]{2,1,0:T(8,128)}) %all-gather.6.cloned.1.call-update) | async-done | bytes 2097168 | tf_op jit(solution)/shard_map/all_gather | solution.py:11
  61.9 8.5 %while.14 = (s32[]{:T(128)}, f32[4,128,128]{2,1,0:T(8,128)S(1)}, s32[]{:T(128)}, f32[8,4,128,128]{3,2,1,0:T(8,128)}, s32[]{:T(128)}, /*index=5*/s32[]{:T(128)}) while((s32[]{:T(128)}, f32[4,128,128]{2,1,0:T(8,128)S(1)}, s32[]{:T(128)}, f32[8,4,128,128]{3,2,1,0:T(8,128)}, s32[]{:T(128)}, /*index=5*/s32[]{:T(128)}) %tuple.40), condition=%wide.region_1.2_spmd.clone, body=%wide.region_0.1_spmd.clone.sunk | while | flops 196612 | bytes 786525 | solution.py:19
  61.9 1.0 add_select_fusion.2
  62.9 1.0 add_select_fusion.2
  64.0 1.0 add_select_fusion.2
  65.1 1.0 add_select_fusion.2
  66.1 1.0 add_select_fusion.2
  67.2 1.0 add_select_fusion.2
  68.3 1.0 add_select_fusion.2
  69.3 1.1 add_select_fusion.2
  70.8 2.4 %multiply_reduce_fusion = (f32[512]{0:T(512)S(1)}, f32[512,4,128]{0,2,1:T(8,128)S(1)}) fusion(f32[512,4,128]{0,2,1:T(8,128)S(1)} %fusion.7, bf16[512,4,128]{0,2,1:T(8,128)(2,1)S(1)} %bitcast.47, pred[512,512]{1,0:T(8,128)(4,1)S(1)} %iota_compare_fusion, bf16[512,512]{1,0:T(8,128)(2,1)} %param.9, bf16[512,512]{1,0:T(8,128)(2,1)S(1)} %copy-done), kind=kOutput, calls=%fused_computation.16 | convolution fusion | flops 540802560 | bytes 3934208 | tf_op jit(solution)/shard_map/hts,she->the/dot_general | solution.py:37
  73.5 1.4 fusion.12
  75.0 8.6 %collective-permute-done = bf16[512,512]{1,0:T(8,128)(2,1)S(1)} collective-permute-done((bf16[512,512]{1,0:T(8,128)(2,1)S(1)}, bf16[512,512]{1,0:T(8,128)(2,1)S(1)}, u32[]{:S(2)}, u32[]{:S(2)}) %collective-permute-start) | collective-permute-done | bytes 524320 | tf_op jit(solution)/shard_map/ppermute | solution.py:63
  83.6 8.6 %collective-permute-done.1 = bf16[512,512]{1,0:T(8,128)(2,1)S(1)} collective-permute-done((bf16[512,512]{1,0:T(8,128)(2,1)S(1)}, bf16[512,512]{1,0:T(8,128)(2,1)S(1)}, u32[]{:S(2)}, u32[]{:S(2)}) %collective-permute-start.1) | collective-permute-done | bytes 524320 | tf_op jit(solution)/shard_map/ppermute | solution.py:63
  92.2 9.5 %psum.7 = f32[512]{0:T(512)S(1)} all-reduce(f32[512]{0:T(512)S(1)} %get-tuple-element.108), channel_id=1, replica_groups=mesh['seq'=8,'head'=4] {'head'}, use_global_device_ids=true, to_apply=%region_3.4 | all-reduce | flops 512 | bytes 4096 | tf_op jit(solution)/shard_map/psum | solution.py:60
  101.7 0.9 constant_dynamic-update-slice_fusion.7
  103.5 0.9 constant_dynamic-update-slice_fusion.5
  104.5 0.9 constant_dynamic-update-slice_fusion.4
  105.4 0.9 constant_dynamic-update-slice_fusion.3
  107.1 0.9 constant_dynamic-update-slice_fusion.1
  108.9 26.5 %all-gather.4.cloned.1.call-done = bf16[2048,1024]{1,0:T(8,128)(2,1)} async-done(((bf16[256,1024]{1,0:T(8,128)(2,1)}), bf16[2048,1024]{1,0:T(8,128)(2,1)}) %all-gather.4.cloned.1.call-update) | async-done | bytes 4194320 | tf_op jit(solution)/shard_map/all_gather | solution.py:67
  135.4 6.1 %multiply_convert_fusion = bf16[512,1024]{1,0:T(8,128)(2,1)} fusion(bf16[2048,1024]{1,0:T(8,128)(2,1)} %all-gather.4.cloned.1.call-done, bf16[512,4096]{1,0:T(8,128)(2,1)} %constant_dynamic-update-slice_fusion, s32[]{:T(128)S(6)} %select_n.40, f32[512]{0:T(512)S(1)} %add_rsqrt_fusion), kind=kOutput, calls=%fused_computation.2 | convolution fusion | flops 2148532224 | bytes 7342084 | tf_op jit(solution)/shard_map/dot_general | solution.py:68
  (18 shorter events, 4.2 us)
Async XLA Ops:
  6.5 63.9 %copy-start = (bf16[512,512]{1,0:T(8,128)(2,1)S(1)}, bf16[512,512]{1,0:T(8,128)(2,1)}, u32[]{:S(2)}) copy-start(bf16[512,512]{1,0:T(8,128)(2,1)} %param.7) | copy-start | bytes 1572868
  6.5 55.3 %all-gather.6.cloned.1.call-start = ((), (), s32[]{:S(2)}) async-start(), calls=%async_computation.1 | async-start | bytes 2359296 | tf_op jit(solution)/shard_map/all_gather | solution.py:11
  9.9 125.4 %all-gather.4.cloned.1.call-start = ((), (), s32[]{:S(2)}) async-start(), calls=%async_computation | async-start | bytes 4718592 | tf_op jit(solution)/shard_map/all_gather | solution.py:67
  74.9 8.7 %collective-permute-start = (bf16[512,512]{1,0:T(8,128)(2,1)S(1)}, bf16[512,512]{1,0:T(8,128)(2,1)S(1)}, u32[]{:S(2)}, u32[]{:S(2)}) collective-permute-start(bf16[512,512]{1,0:T(8,128)(2,1)S(1)} %fusion.12), channel_id=1, source_target_pairs={{0,1},{1,2},{2,3},{3,0},{4,5},{5,6},{6,7},{7,4},{8,9},{9,10},{10,1... | collective-permute-start | bytes 1572872 | tf_op jit(solution)/shard_map/ppermute | solution.py:63
  83.5 8.6 %collective-permute-start.1 = (bf16[512,512]{1,0:T(8,128)(2,1)S(1)}, bf16[512,512]{1,0:T(8,128)(2,1)S(1)}, u32[]{:S(2)}, u32[]{:S(2)}) collective-permute-start(bf16[512,512]{1,0:T(8,128)(2,1)S(1)} %collective-permute-done), channel_id=1, source_target_pairs={{0,1},{1,2},{2,3},{3,0},{4,5},{5,6},{6,7},{7,4},{8,9},{9,10},{10,1... | collective-permute-start | bytes 1572872 | tf_op jit(solution)/shard_map/ppermute | solution.py:63
  92.2 9.6 %collective-permute-start.2 = (bf16[512,512]{1,0:T(8,128)(2,1)S(1)}, bf16[512,512]{1,0:T(8,128)(2,1)S(1)}, u32[]{:S(2)}, u32[]{:S(2)}) collective-permute-start(bf16[512,512]{1,0:T(8,128)(2,1)S(1)} %collective-permute-done.1), channel_id=1, source_target_pairs={{0,1},{1,2},{2,3},{3,0},{4,5},{5,6},{6,7},{7,4},{8,9},{9,10},{10,1... | collective-permute-start | bytes 1572872 | tf_op jit(solution)/shard_map/ppermute | solution.py:63
Sparse Core Ops, SparseCore 0:
  10.0 51.7 all-gather.5
  64.0 71.3 all-gather.3
